TPU v7x, 32 devices: a whole 2x2x4 slice. The times are simulated.
32 devices in a mesh: grp: 8 (over y, x, core), fsdp: 4 (over z).
Axes of the slice: x: 2, y: 2, z: 4, core: 2. Of those that a mesh axis runs over, the one named last changes fastest.
Arguments:
- layer_inputs: bfloat16 [8, 2048, 2048], P('grp', 'fsdp'), may hold values from -6 to 6
- key_cotangent: bfloat16 [8, 2048, 768], P('grp', 'fsdp'), may hold values from -0.099609375 to 0.099609375
- key_weights: bfloat16 [2048, 768], P('fsdp'), may hold values from -0.125 to 0.125
- outer_momentum: float32 [2048, 768], P('fsdp'), may hold values from -0.02 to 0.02
- state_codes: int32 [8, 2048, 768], P('grp', 'fsdp'), may hold values from 0 to 255
- first_row_max: float32 [8, 2048], P('grp', 'fsdp'), may hold values from 0.1 to 2
- first_col_max: float32 [8, 768], P('grp'), may hold values from 0.1 to 2
- second_row_max: float32 [8, 2048], P('grp', 'fsdp'), may hold values from 0.1 to 4
- second_col_max: float32 [8, 768], P('grp'), may hold values from 0.1 to 4
Outputs:
- new_weights: float32 [2048, 768], P('fsdp')
- new_momentum: float32 [2048, 768], P('fsdp')
- first_state: bfloat16 [8, 2048, 768], P('grp', 'fsdp')
- second_state: bfloat16 [8, 2048, 768], P('grp', 'fsdp')
- new_first_row_max: float32 [8, 2048], P('grp', 'fsdp')
- new_first_col_max: float32 [8, 768], P('grp')
- new_second_row_max: float32 [8, 2048], P('grp', 'fsdp')
- new_second_col_max: float32 [8, 768], P('grp')
- next_keys: bfloat16 [8, 2048, 768], P('grp', 'fsdp')
All inputs are finite; a program needn't handle non-finite values. Where the computation divides by a largest or mean magnitude, that divisor is 1e-20 or more.
Results may differ from a plain program's by a relative error of at most 0.018.
Values may be sent and summed in bfloat16 or wider, within the bound.
A program may use at most 64 MiB of HBM per device.

v0:
```python
import jax
import jax.numpy as jnp
from jax import lax
from jax.sharding import PartitionSpec as P

beta_one = 0.9
beta_two = 0.95
bias_one = 1.0 - 0.9**10
bias_two = 1.0 - 0.95**10
adam_eps = 1e-08
inner_rate = 0.01
weight_decay = 0.1
outer_rate = 0.7
outer_beta = 0.9
stat_eps = 1e-06


def local(
    layer_inputs,
    key_cotangent,
    key_weights,
    outer_momentum,
    state_codes,
    first_row_max,
    first_col_max,
    second_row_max,
    second_col_max,
):
    tokens = layer_inputs[0]
    cotangent = key_cotangent[0]
    columns = tokens
    gradient = lax.psum_scatter(
        lax.dot_general(
            columns, cotangent, (((0,), (0,)), ((), ())), preferred_element_type=jnp.float32
        ).astype(jnp.bfloat16),
        "fsdp",
        scatter_dimension=0,
        tiled=True,
    ).astype(jnp.float32)
    packed_codes = state_codes[0]
    first_code = (packed_codes // 16).astype(jnp.float32)
    second_code = (packed_codes % 16).astype(jnp.float32)
    first_old = (
        jnp.minimum(first_row_max[0][:, None], first_col_max[0][None, :]) * (first_code - 7.5) / 7.5
    )
    second_old = (
        jnp.minimum(second_row_max[0][:, None], second_col_max[0][None, :])
        * ((second_code + 1.0) / 16.0) ** 2
    )
    first_new = beta_one * first_old + (1.0 - beta_one) * gradient
    second_new = beta_two * second_old + (1.0 - beta_two) * gradient * gradient
    weights_float = key_weights.astype(jnp.float32)
    update = first_new / bias_one / (jnp.sqrt(second_new / bias_two) + adam_eps)
    pseudo_grad = inner_rate * (update + weight_decay * weights_float)
    first_rmax = jnp.max(jnp.abs(first_new), axis=1) + stat_eps
    second_rmax = jnp.max(second_new, axis=1) + stat_eps
    first_local = jnp.max(jnp.abs(first_new), axis=0)
    second_local = jnp.max(second_new, axis=0)
    first_cmax, second_cmax = lax.pmax((first_local, second_local), "fsdp")
    first_cmax = first_cmax + stat_eps
    second_cmax = second_cmax + stat_eps
    first_state = (first_new / jnp.minimum(first_rmax[:, None], first_cmax[None, :])).astype(
        jnp.bfloat16
    )
    second_state = (second_new / jnp.minimum(second_rmax[:, None], second_cmax[None, :])).astype(
        jnp.bfloat16
    )
    group_count = lax.axis_size("grp")
    averaged = lax.psum(pseudo_grad, "grp") / group_count
    momentum = outer_beta * outer_momentum + averaged
    new_weights = weights_float - outer_rate * (averaged + outer_beta * momentum)
    weights_half = new_weights.astype(jnp.bfloat16)
    columns = tokens
    next_keys = jnp.dot(
        columns,
        lax.all_gather(weights_half, "fsdp", axis=0, tiled=True),
        preferred_element_type=jnp.float32,
    )
    return (
        new_weights,
        momentum,
        first_state[None],
        second_state[None],
        first_rmax[None],
        first_cmax[None],
        second_rmax[None],
        second_cmax[None],
        next_keys.astype(jnp.bfloat16)[None],
    )


def solution(mesh):
    return jax.shard_map(
        local,
        mesh=mesh,
        in_specs=(
            P("grp", "fsdp", None),
            P("grp", "fsdp", None),
            P("fsdp", None),
            P("fsdp", None),
            P("grp", "fsdp", None),
            P("grp", "fsdp"),
            P("grp", None),
            P("grp", "fsdp"),
            P("grp", None),
        ),
        out_specs=(
            P("fsdp", None),
            P("fsdp", None),
            P("grp", "fsdp", None),
            P("grp", "fsdp", None),
            P("grp", "fsdp"),
            P("grp", None),
            P("grp", "fsdp"),
            P("grp", None),
            P("grp", "fsdp", None),
        ),
        check_vma=False,
    )
```

profile of v0, /device:TPU:0, one launch (start us, length us, event | category | flops | bytes accessed | tf_op | source)
XLA Modules:
  0.0 233.3 jit_solution(150988136328190076)
XLA Ops:
  7.2 0.0 copy-start
  7.2 0.0 reduce-scatter.2.cloned.1.call-start
  7.2 1.5 copy-done
  8.8 4.6 %convolution_convert_fusion = bf16[2048,768]{1,0:T(8,128)(2,1)} fusion(bf16[1,512,2048]{2,1,0:T(8,128)(2,1)S(1)} %copy-done, bf16[1,512,768]{2,1,0:T(8,128)(2,1)} %param.10), kind=kOutput, calls=%fused_computation | convolution fusion | flops 1612185600 | bytes 6029312 | tf_op jit(solution)/shard_map/dot_general | solution.py:33
  13.4 0.0 copy-start.4
  13.4 0.0 copy-start.5
  13.4 0.0 copy-start.6
  13.4 0.0 copy-start.7
  13.4 0.0 reduce-scatter.2.cloned.1.call-update
  13.4 0.0 all-reduce.3.cloned.1.call-start
  13.5 0.6 copy-done.4
  14.1 0.0 copy-done.5
  14.1 62.6 %reduce-scatter.2.cloned.1.call-done = bf16[512,768]{1,0:T(8,128)(2,1)} async-done(((bf16[2048,768]{1,0:T(8,128)(2,1)}), bf16[512,768]{1,0:T(8,128)(2,1)}) %reduce-scatter.2.cloned.1.call-update) | async-done | bytes 786448 | tf_op jit(solution)/shard_map/reduce_scatter | solution.py:32
  76.7 0.0 copy-done.6
  76.7 0.0 copy-done.7
  76.7 0.0 copy-start.1
  76.8 5.3 %abs_reduce_fusion.1 = (f32[512]{0:T(512)S(1)}, f32[768]{0:T(1024)S(1)}, f32[512,768]{1,0:T(8,128)}, f32[768]{0:T(1024)S(1)}, f32[512]{0:T(512)S(1)}, /*index=5*/f32[512,768]{1,0:T(8,128)}) fusion(bf16[512,768]{1,0:T(8,128)(2,1)} %reduce-scatter.2.cloned.1.call-done, s32[1,512,768]{2,1,0:T(8,128)} %param.13, f32[768]{0:T(1024)S(1)} %reduce, ...), kind=kLoop, calls=%fused_computation.35 | loop fusion | flops 16512512 | bytes 5525504 | tf_op jit(solution)/shard_map/reduce_max | solution.py:55
  82.0 0.0 copy-start.2
  82.0 0.0 copy-start.3
  82.1 10.5 %all-reduce = (f32[768]{0:T(1024)S(1)}, f32[768]{0:T(1024)S(1)}) all-reduce(f32[768]{0:T(1024)S(1)} %get-tuple-element.21, f32[768]{0:T(1024)S(1)} %get-tuple-element.29), channel_id=1, replica_groups=mesh['grp'=8,'fsdp'=4] {'fsdp'}, use_global_device_ids=true, to_apply=%region_4.5 | all-reduce | flops 1536 | bytes 12288 | tf_op jit(solution)/shard_map/pmax | solution.py:59
  92.6 0.0 copy-done.1
  92.6 4.7 %fusion.28 = (bf16[1,512,768]{2,1,0:T(8,128)(2,1)}, f32[512,768]{1,0:T(8,128)}, bf16[1,512,768]{2,1,0:T(8,128)(2,1)}) fusion(f32[512,768]{1,0:T(8,128)} %get-tuple-element.31, f32[768]{0:T(1024)S(1)} %get-tuple-element.37, f32[512]{0:T(512)S(1)} %get-tuple-element.35, bf16[512,768]{1,0:T(8,128)(2,1)S(1)} %copy-done.1, f32[512,768]{1,0:T(8,128)} %get-tuple-element.28, ...), kind=kLoop, calls=%fused_computation.41 | loop fusion | flops 5505024 | bytes 7088128 | tf_op jit(solution)/shard_map/broadcast_in_dim | solution.py:83
  97.3 0.0 copy-done.2
  97.3 0.0 copy-done.3
  97.3 0.0 all-reduce.3.cloned.1.call-update
  97.4 0.0 all-gather.2.cloned.1.call-start
  97.4 57.3 %all-reduce.3.cloned.1.call-done = f32[512,768]{1,0:T(8,128)} async-done(((f32[512,768]{1,0:T(8,128)}), f32[512,768]{1,0:T(8,128)}) %all-reduce.3.cloned.1.call-update) | async-done | bytes 1572880 | tf_op jit(solution)/shard_map/psum | solution.py:69
  154.7 4.3 %fusion.30 = (bf16[512,768]{1,0:T(8,128)(2,1)}, f32[512,768]{1,0:T(8,128)}, f32[512,768]{1,0:T(8,128)}) fusion(f32[512,768]{1,0:T(8,128)} %all-reduce.3.cloned.1.call-done, bf16[512,768]{1,0:T(8,128)(2,1)S(1)} %copy-done.1, f32[512,768]{1,0:T(8,128)} %param.12), kind=kLoop, calls=%fused_computation.47 | loop fusion | flops 3538944 | bytes 7864320 | tf_op jit(solution)/shard_map/convert_element_type | solution.py:72
  158.9 0.0 all-gather.2.cloned.1.call-update
  159.0 0.6 broadcast_in_dim.23
  159.5 0.6 broadcast_in_dim.24
  160.1 61.8 %all-gather.2.cloned.1.call-done = bf16[2048,768]{1,0:T(8,128)(2,1)} async-done(((bf16[512,768]{1,0:T(8,128)(2,1)}), bf16[2048,768]{1,0:T(8,128)(2,1)}) %all-gather.2.cloned.1.call-update) | async-done | bytes 3145744 | tf_op jit(solution)/shard_map/all_gather | solution.py:76
  221.9 3.7 %fusion.22 = bf16[1,512,768]{1,2,0:T(8,128)(2,1)S(1)} fusion(bf16[2048,768]{1,0:T(8,128)(2,1)} %all-gather.2.cloned.1.call-done, bf16[1,512,2048]{2,1,0:T(8,128)(2,1)S(1)} %copy-done), kind=kOutput, calls=%fused_computation.37 | convolution fusion | flops 1611005952 | bytes 6029312 | tf_op jit(solution)/shard_map/dot_general | solution.py:74
  225.6 1.2 copy.18
  (4 shorter events, 0.0 us)
Async XLA Ops:
  7.2 1.6 copy-start
  7.2 69.6 %reduce-scatter.2.cloned.1.call-start = ((), (), s32[]{:S(2)}) async-start(), calls=%async_computation.1 | async-start | bytes 3932160 | tf_op jit(solution)/shard_map/reduce_scatter | solution.py:32
  13.4 0.7 copy-start.4
  13.4 0.7 copy-start.5
  13.4 63.3 %copy-start.6 = (f32[1,512]{1,0:T(1,128)S(1)}, f32[1,512]{1,0:T(1,128)}, u32[]{:S(2)}) copy-start(f32[1,512]{1,0:T(1,128)} %param.14) | copy-start | bytes 6148
  13.4 63.3 %copy-start.7 = (f32[1,512]{1,0:T(1,128)S(1)}, f32[1,512]{1,0:T(1,128)}, u32[]{:S(2)}) copy-start(f32[1,512]{1,0:T(1,128)} %param.16) | copy-start | bytes 6148
  13.4 141.2 %all-reduce.3.cloned.1.call-start = ((), (), s32[]{:S(2)}) async-start(), calls=%async_computation.2 | async-start | bytes 3145728 | tf_op jit(solution)/shard_map/psum | solution.py:69
  76.7 15.9 %copy-start.1 = (bf16[512,768]{1,0:T(8,128)(2,1)S(1)}, bf16[512,768]{1,0:T(8,128)(2,1)}, u32[]{:S(2)}) copy-start(bf16[512,768]{1,0:T(8,128)(2,1)} %param.11) | copy-start | bytes 2359300
  82.0 15.3 %copy-start.2 = (f32[512]{0:T(512)}, f32[512]{0:T(512)S(1)}, u32[]{:S(2)}) copy-start(f32[512]{0:T(512)S(1)} %get-tuple-element.35) | copy-start | bytes 6148
  82.0 15.3 %copy-start.3 = (f32[512]{0:T(512)}, f32[512]{0:T(512)S(1)}, u32[]{:S(2)}) copy-start(f32[512]{0:T(512)S(1)} %get-tuple-element.36) | copy-start | bytes 6148
  97.4 124.5 %all-gather.2.cloned.1.call-start = ((), (), s32[]{:S(2)}) async-start(), calls=%async_computation.3 | async-start | bytes 3932160 | tf_op jit(solution)/shard_map/all_gather | solution.py:76
Sparse Core Ops, SparseCore 0:
  13.6 63.1 reduce-scatter.1
  97.5 57.1 all-reduce.2
  159.1 62.7 all-gather.1
where the time goes:
time: 234 us; the launch traced here: 233 us
  waiting for transfers between devices  182 us (78%)
  other arithmetic  14.3 us (6%)
  between operations  13.8 us (6%)
  blocking collectives  10.5 us (4%)
  matrix products  8.36 us (4%)
  local copies, waits for them, and re-layouts  4.48 us (2%)
    reduce_scatter x1, waiting for transfers between devices, local(): lax.psum_scatter(lax.dot_general(columns, cotangent, (((0,), (0,)), ((),...  62.6 us
    all_gather x1, waiting for transfers between devices, local(): lax.all_gather(weights_half, 'fsdp', axis=0, tiled=True)  61.8 us
    psum x1, waiting for transfers between devices, local(): averaged = lax.psum(pseudo_grad, 'grp') / group_count  57.3 us
    pmax x1, blocking collectives, local(): first_cmax, second_cmax = lax.pmax((first_local, second_local), 'fsdp')  10.5 us
    reduce_max x1, other arithmetic, local(): first_rmax = jnp.max(jnp.abs(first_new), axis=1) + stat_eps  5.29 us
    broadcast_in_dim x1, other arithmetic, local(): second_state[None]  4.73 us
  transfers between devices with their start and end apart: 3, of which 3 were waited for; matrix products, arithmetic and copies ran while one was open for 1% of the time, Pallas kernels for 0%

commit v1 on v0

v1 whole, which is shorter than its diff:
```python
import functools
import jax
import jax.numpy as jnp
from jax import lax
from jax.experimental import pallas as pl
from jax.experimental.pallas import tpu as pltpu
from jax.sharding import PartitionSpec as P

MESH = pl.DeviceIdType.MESH
f32, bf16 = jnp.float32, jnp.bfloat16
beta_one = 0.9
beta_two = 0.95
bias_one = 1.0 - 0.9**10
bias_two = 1.0 - 0.95**10
adam_eps = 1e-08
inner_rate = 0.01
weight_decay = 0.1
outer_rate = 0.7
outer_beta = 0.9
stat_eps = 1e-06
TILE = 16


def to_column(row):
    return jnp.broadcast_to(row, (128, row.shape[1])).T[:, :1]


def to_row(column):
    return jnp.broadcast_to(column, (column.shape[0], 128)).T[:1, :]


def kernel(
    n, G, S, R, PR, NP,
    x_hbm, c_hbm, w_hbm, m_hbm, q_hbm, frm, fcm, srm, scm,
    o_w, o_m, o_fs, o_ss, o_frm, o_fcm, o_srm, o_scm, o_k,
    x, ct, w, m, q, tb, rb, pb, rp, av, wf, fn, sn, acc, fcol, scol, frn, srn, ca, cb, cmb,
    ld, ts, tr, ps, pr, as_, ar, gs, gr, hs, hr, cs, cr,
):
    g = lax.axis_index("grp")
    z = lax.axis_index("fsdp")
    rows = S * R
    C = w.shape[1]
    half = R // 2
    h = lax.rem(g, 2)
    mate = g + 1 - 2 * h

    loads = [
        pltpu.make_async_copy(src, dst, ld.at[i])
        for i, (src, dst) in enumerate(
            ((c_hbm, ct), (x_hbm, x), (q_hbm, q), (w_hbm, w), (m_hbm, m))
        )
    ]
    for load in loads:
        load.start()

    barrier = pltpu.get_barrier_semaphore()
    for d in range(1, G):
        pl.semaphore_signal(
            barrier, inc=1, device_id=(lax.rem(g + d, G), z), device_id_type=MESH
        )
    for d in range(1, n):
        pl.semaphore_signal(
            barrier, inc=1, device_id=(g, lax.rem(z + d, n)), device_id_type=MESH
        )

    for s in range(S):
        block = pl.ds(s * R, R)
        fcol[block, :] = to_column(frm[:, block])
        scol[block, :] = to_column(srm[:, block])
    ca[...] = jnp.zeros_like(ca)
    cb[...] = jnp.zeros_like(cb)

    pl.semaphore_wait(barrier, G - 1 + n - 1)
    loads[0].wait()
    loads[1].wait()

    def term(c, s):
        columns = pl.ds(pl.multiple_of(c * rows + s * R, 128), R)
        return lax.dot_general(
            x[:, columns], ct[...], (((0,), (0,)), ((), ())), preferred_element_type=f32
        )

    def move(s, c, slot, to):
        return pltpu.make_async_remote_copy(
            src_ref=tb.at[s, c], dst_ref=rb.at[s, slot], send_sem=ts.at[s, c],
            recv_sem=tr.at[s, slot], device_id=(g, to), device_id_type=MESH,
        )

    other_z = lax.rem(z + 1, n)

    def stream(s):
        def step(k, carry):
            right = n - 1 - k
            left = k

            @pl.when(right > z)
            def _():
                @pl.when(z == 0)
                def _():
                    tb[s, right] = term(right, s).astype(bf16)

                @pl.when(z > 0)
                def _():
                    own = term(right, s)
                    move(s, right, right, other_z).wait_recv()
                    tb[s, right] = (own + rb[s, right].astype(f32)).astype(bf16)

                move(s, right, right, z + 1).start()

            @pl.when(left < z)
            def _():
                @pl.when(z == n - 1)
                def _():
                    tb[s, left] = term(left, s).astype(bf16)

                @pl.when(z < n - 1)
                def _():
                    own = term(left, s)
                    move(s, left, left, other_z).wait_recv()
                    tb[s, left] = (own + rb[s, left].astype(f32)).astype(bf16)

                move(s, left, jnp.where(left == z - 1, n, left), z - 1).start()

            return carry

        lax.fori_loop(0, n - 1, step, 0)

    def piece(s, p, to):
        return pltpu.make_async_remote_copy(
            src_ref=pb.at[s, p], dst_ref=rp.at[s, g], send_sem=ps.at[s, p],
            recv_sem=pr.at[s, g], device_id=(to, z), device_id_type=MESH,
        )

    def piece_from(s, p):
        return pltpu.make_async_remote_copy(
            src_ref=pb.at[s, 0], dst_ref=rp.at[s, p], send_sem=ps.at[s, 0],
            recv_sem=pr.at[s, p], device_id=(mate, z), device_id_type=MESH,
        )

    def inner(s):
        acc[pl.ds(0, R), :] = term(z, s)

        @pl.when(z > 0)
        def _():
            move(s, z, z, other_z).wait_recv()
            acc[pl.ds(0, R), :] += rb[s, z].astype(f32)

        @pl.when(z < n - 1)
        def _():
            move(s, z, n, other_z).wait_recv()
            acc[pl.ds(0, R), :] += rb[s, n].astype(f32)

        def tile(i, carry):
            at = pl.multiple_of(i * TILE, TILE)
            place = pl.ds(pl.multiple_of(s * R + i * TILE, TILE), TILE)
            gradient = acc[pl.ds(at, TILE), :]
            codes = q[place, :]
            first_code = (codes >> 4).astype(f32)
            second_code = (codes & 15).astype(f32)
            first_old = jnp.minimum(fcol[place, :], fcm[...]) * ((first_code - 7.5) / 7.5)
            level = (second_code + 1.0) * (1.0 / 16.0)
            second_old = jnp.minimum(scol[place, :], scm[...]) * (level * level)
            first_new = beta_one * first_old + (1.0 - beta_one) * gradient
            second_new = beta_two * second_old + (1.0 - beta_two) * gradient * gradient
            fn[place, :] = first_new
            sn[place, :] = second_new
            update = (first_new / bias_one) / (jnp.sqrt(second_new / bias_two) + adam_eps)
            pseudo = inner_rate * (update + weight_decay * w[place, :].astype(f32))
            pb[s, i // (PR // TILE), pl.ds(lax.rem(i, PR // TILE) * TILE, TILE), :] = pseudo.astype(bf16)
            size = jnp.abs(first_new)
            ca[...] = jnp.maximum(ca[...], size)
            cb[...] = jnp.maximum(cb[...], second_new)
            frn[place, :] = jnp.max(size, axis=1, keepdims=True) + stat_eps
            srn[place, :] = jnp.max(second_new, axis=1, keepdims=True) + stat_eps
            return carry

        lax.fori_loop(0, R // TILE, tile, 0)

        def send(d, carry):
            p = lax.rem(g + d, G)

            @pl.when(p < NP)
            def _():
                piece(s, p, p).start()

            return carry

        lax.fori_loop(1, G, send, 0)

    def share(s, p, to):
        own = pl.ds(pl.multiple_of(p * PR, PR), PR)
        return pltpu.make_async_remote_copy(
            src_ref=av.at[s, own], dst_ref=av.at[s, own], send_sem=as_.at[s, to],
            recv_sem=ar.at[s, p], device_id=(to, z), device_id_type=MESH,
        )

    def reduce(s):
        @pl.when(g < NP)
        def _():
            acc[pl.ds(0, PR), :] = pb[s, g].astype(f32)

            def add(d, carry):
                p = lax.rem(g + d, G)
                piece_from(s, p).wait_recv()
                acc[pl.ds(0, PR), :] += rp[s, p].astype(f32)
                return carry

            lax.fori_loop(1, G, add, 0)
            av[s, pl.ds(pl.multiple_of(g * PR, PR), PR), :] = (
                acc[pl.ds(0, PR), :] * (1.0 / G)
            ).astype(bf16)

            def send(d, carry):
                share(s, g, lax.rem(g + d, G)).start()
                return carry

            lax.fori_loop(1, G, send, 0)

    def relay(s, c, way, to):
        part = pl.ds(pl.multiple_of(s * R + h * half, half), half)
        return pltpu.make_async_remote_copy(
            src_ref=wf.at[c, part], dst_ref=wf.at[c, part], send_sem=gs.at[way, s, c],
            recv_sem=gr.at[s, c], device_id=(g, to), device_id_type=MESH,
        )

    def hand(s, c):
        part = pl.ds(pl.multiple_of(s * R + h * half, half), half)
        return pltpu.make_async_remote_copy(
            src_ref=wf.at[c, part], dst_ref=wf.at[c, part], send_sem=hs.at[s, c],
            recv_sem=hr.at[s, c], device_id=(mate, z), device_id_type=MESH,
        )

    def hand_from(s, c):
        part = pl.ds(pl.multiple_of(s * R + (1 - h) * half, half), half)
        return pltpu.make_async_remote_copy(
            src_ref=wf.at[c, part], dst_ref=wf.at[c, part], send_sem=hs.at[s, c],
            recv_sem=hr.at[s, c], device_id=(mate, z), device_id_type=MESH,
        )

    def outer(s):
        def wait(p, carry):
            @pl.when(p != g)
            def _():
                share(s, p, mate).wait_recv()

            return carry

        lax.fori_loop(0, NP, wait, 0)

        def tile(i, carry):
            place = pl.ds(pl.multiple_of(s * R + i * TILE, TILE), TILE)
            averaged = av[s, pl.ds(pl.multiple_of(i * TILE, TILE), TILE), :].astype(f32)
            momentum = outer_beta * m[place, :] + averaged
            fresh = w[place, :].astype(f32) - outer_rate * (averaged + outer_beta * momentum)
            o_m[place, :] = momentum
            o_w[place, :] = fresh
            wf[z, place, :] = fresh.astype(bf16)
            return carry

        lax.fori_loop(0, R // TILE, tile, 0)

        @pl.when(z < n - 1)
        def _():
            relay(s, z, 0, z + 1).start()

        @pl.when(z > 0)
        def _():
            relay(s, z, 1, z - 1).start()

    def hop(s, j):
        @pl.when(z - j >= 0)
        def _():
            c = z - j
            relay(s, c, 0, other_z).wait_recv()

            @pl.when(z < n - 1)
            def _():
                relay(s, c, 0, z + 1).start()

            hand(s, c).start()

        @pl.when(z + j < n)
        def _():
            c = z + j
            relay(s, c, 1, other_z).wait_recv()

            @pl.when(z > 0)
            def _():
                relay(s, c, 1, z - 1).start()

            hand(s, c).start()

    def hops(u):
        for j in range(1, n):
            if (u - 3 - j) % 2 == 0 and 0 <= (u - 3 - j) // 2 < S:
                hop((u - 3 - j) // 2, j)

    @pl.when((z == 0) | (z == n - 1))
    def _():
        def every(s, carry):
            stream(s)
            return carry

        lax.fori_loop(0, S, every, 0)

    for load in loads[2:]:
        load.wait()

    def column_max(slot, to):
        return pltpu.make_async_remote_copy(
            src_ref=cmb.at[z], dst_ref=cmb.at[z], send_sem=cs.at[slot],
            recv_sem=cr.at[z], device_id=(g, to), device_id_type=MESH,
        )

    def column_max_from(c):
        return pltpu.make_async_remote_copy(
            src_ref=cmb.at[c], dst_ref=cmb.at[c], send_sem=cs.at[0],
            recv_sem=cr.at[c], device_id=(g, other_z), device_id_type=MESH,
        )

    for s in range(S + 1):
        if s < S:
            @pl.when((z > 0) & (z < n - 1))
            def _():
                stream(s)
        hops(2 * s)
        if s >= 1:
            reduce(s - 1)
        if s < S:
            inner(s)
        if s == S - 1:
            cmb[z, pl.ds(0, 1), :] = jnp.max(ca[...], axis=0, keepdims=True)
            cmb[z, pl.ds(1, 1), :] = jnp.max(cb[...], axis=0, keepdims=True)
            for d in range(1, n):
                column_max(d, lax.rem(z + d, n)).start()
        if s >= 1:
            outer(s - 1)
        hops(2 * s + 1)

    for d in range(1, n):
        column_max_from(lax.rem(z + d, n)).wait_recv()
    scales = jnp.max(cmb[...], axis=0) + stat_eps
    o_fcm[...] = scales[0:1]
    o_scm[...] = scales[1:2]

    def states(s):
        def tile(i, carry):
            place = pl.ds(pl.multiple_of(s * R + i * TILE, TILE), TILE)
            o_fs[place, :] = (fn[place, :] / jnp.minimum(frn[place, :], o_fcm[...])).astype(bf16)
            o_ss[place, :] = (sn[place, :] / jnp.minimum(srn[place, :], o_scm[...])).astype(bf16)
            return carry

        lax.fori_loop(0, R // TILE, tile, 0)
        block = pl.ds(s * R, R)
        o_frm[:, block] = to_row(frn[block, :])
        o_srm[:, block] = to_row(srn[block, :])

    for s in range(S):
        states(s)

    def product(c):
        columns = pl.ds(pl.multiple_of(c * rows, 128), rows)
        return jnp.dot(x[:, columns], wf[c], preferred_element_type=f32)

    acc[...] = product(z)
    for u in range(2 * S + 2, 2 * S + 2 + n - 1):
        hops(u)

    def gather(j, carry):
        for c in (z - j, z + j):
            @pl.when((c >= 0) & (c < n))
            def _():
                for s in range(S):
                    hand_from(s, c).wait_recv()
                acc[...] += product(c)
        return carry

    lax.fori_loop(1, n, gather, 0)
    o_k[...] = acc[...].astype(bf16)

    for s in range(S):
        def sent(c, carry):
            @pl.when(c != z)
            def _():
                move(s, c, c, other_z).wait_send()
                hand(s, c).wait_send()

            @pl.when((c <= z) & (z < n - 1))
            def _():
                relay(s, c, 0, other_z).wait_send()

            @pl.when((c >= z) & (z > 0))
            def _():
                relay(s, c, 1, other_z).wait_send()

            return carry

        lax.fori_loop(0, n, sent, 0)

        def plane(p, carry):
            @pl.when(p != g)
            def _():
                @pl.when(p < NP)
                def _():
                    piece(s, p, mate).wait_send()

                @pl.when(g < NP)
                def _():
                    share(s, g, p).wait_send()

            return carry

        lax.fori_loop(0, G, plane, 0)
    for d in range(1, n):
        column_max(d, other_z).wait_send()


def local(x, ct, w, m, q, frm, fcm, srm, scm):
    n, G = lax.axis_size("fsdp"), lax.axis_size("grp")
    rows, C = w.shape
    T, K = x.shape[1:]
    R = min(128, rows)
    S = rows // R
    PR = max(TILE, R // G)
    NP = R // PR
    hbm = pl.BlockSpec(memory_space=pl.ANY)
    vmem = pl.BlockSpec(memory_space=pltpu.VMEM)
    dma = pltpu.SemaphoreType.DMA
    shape = jax.ShapeDtypeStruct
    outs = pl.pallas_call(
        functools.partial(kernel, n, G, S, R, PR, NP),
        out_shape=(
            shape((rows, C), f32), shape((rows, C), f32),
            shape((rows, C), bf16), shape((rows, C), bf16),
            shape((1, rows), f32), shape((1, C), f32),
            shape((1, rows), f32), shape((1, C), f32),
            shape((T, C), bf16),
        ),
        in_specs=[hbm] * 5 + [vmem] * 4,
        out_specs=(vmem,) * 9,
        scratch_shapes=[
            pltpu.VMEM((T, K), bf16), pltpu.VMEM((T, C), bf16), pltpu.VMEM((rows, C), bf16),
            pltpu.VMEM((rows, C), f32), pltpu.VMEM((rows, C), jnp.int32),
            pltpu.VMEM((S, n, R, C), bf16), pltpu.VMEM((S, n + 1, R, C), bf16),
            pltpu.VMEM((S, NP, PR, C), bf16), pltpu.VMEM((S, G, PR, C), bf16),
            pltpu.VMEM((S, R, C), bf16), pltpu.VMEM((n, rows, C), bf16),
            pltpu.VMEM((rows, C), f32), pltpu.VMEM((rows, C), f32), pltpu.VMEM((T, C), f32),
            pltpu.VMEM((rows, 1), f32), pltpu.VMEM((rows, 1), f32),
            pltpu.VMEM((rows, 1), f32), pltpu.VMEM((rows, 1), f32),
            pltpu.VMEM((TILE, C), f32), pltpu.VMEM((TILE, C), f32), pltpu.VMEM((n, 2, C), f32),
            dma((5,)), dma((S, n)), dma((S, n + 1)), dma((S, NP)), dma((S, G)),
            dma((S, G)), dma((S, NP)), dma((2, S, n)), dma((S, n)), dma((S, n)), dma((S, n)),
            dma((n,)), dma((n,)),
        ],
        compiler_params=pltpu.CompilerParams(
            collective_id=0, has_side_effects=True, vmem_limit_bytes=60 * 1024 * 1024
        ),
    )(x[0], ct[0], w, m, q[0], frm, fcm, srm, scm)
    new_w, new_m, fs, ss, nfr, nfc, nsr, nsc, keys = outs
    return new_w, new_m, fs[None], ss[None], nfr, nfc, nsr, nsc, keys[None]


def solution(mesh):
    return jax.shard_map(
        local,
        mesh=mesh,
        in_specs=(
            P("grp", "fsdp", None), P("grp", "fsdp", None), P("fsdp", None), P("fsdp", None),
            P("grp", "fsdp", None), P("grp", "fsdp"), P("grp", None), P("grp", "fsdp"),
            P("grp", None),
        ),
        out_specs=(
            P("fsdp", None), P("fsdp", None), P("grp", "fsdp", None), P("grp", "fsdp", None),
            P("grp", "fsdp"), P("grp", None), P("grp", "fsdp"), P("grp", None),
            P("grp", "fsdp", None),
        ),
        check_vma=False,
    )
```

time: 234 us -> 127 us (0.54)
  waiting for transfers between devices: 182 us -> 0 us
  Pallas kernels: 0 us -> 117 us
  other arithmetic: 14.3 us -> 0 us
  between operations: 13.8 us -> 0.68 us
  blocking collectives: 10.5 us -> 0 us
  matrix products: 8.36 us -> 0 us
  local copies, waits for them, and re-layouts: 4.48 us -> 9.42 us
    pallas_call x0 -> x1, Pallas kernels: none -> 117 us  [local(): pl.pallas_call(functools.partial(kernel, n, G, S, R, PR, NP), out_shape=(...]
    reduce_scatter x1 -> x0, waiting for transfers between devices: 62.6 us -> none  [local(): lax.psum_scatter(lax.dot_general(columns, cotangent, (((0,), (0,)), ((),...]
    all_gather x1 -> x0, waiting for transfers between devices: 61.8 us -> none  [local(): lax.all_gather(weights_half, 'fsdp', axis=0, tiled=True)]
    psum x1 -> x0, waiting for transfers between devices: 57.3 us -> none  [local(): averaged = lax.psum(pseudo_grad, 'grp') / group_count]
    pmax x1 -> x0, blocking collectives: 10.5 us -> none  [local(): first_cmax, second_cmax = lax.pmax((first_local, second_local), 'fsdp')]
    dot_general x2 -> x0, matrix products: 8.36 us -> none  [the longest x1 4.64 us: local(): lax.dot_general(columns, cotangent, (((0,), (0,)), ((), ())), preferred_e...]
    unnamed x17 -> x25, local copies, waits for them, and re-layouts: 3.32 us -> 9.42 us
    reduce_max x1 -> x0, other arithmetic: 5.29 us -> none  [local(): first_rmax = jnp.max(jnp.abs(first_new), axis=1) + stat_eps]
  transfers between devices with their start and end apart: 3 -> 0, of which waited for: 3 -> 0; matrix products, arithmetic and copies ran while one was open for 1% -> 0% of each run, Pallas kernels for 0% -> 0%
where the time goes in v1:
time: 127 us
  Pallas kernels  117 us (92%)
  local copies, waits for them, and re-layouts  9.42 us (7%)
    pallas_call x1, Pallas kernels, local(): pl.pallas_call(functools.partial(kernel, n, G, S, R, PR, NP), out_shape=(...  117 us
    unnamed x25, local copies, waits for them, and re-layouts  9.42 us

profile of v1, /device:TPU:0, one launch (start us, length us, event | category | flops | bytes accessed | tf_op | source)
XLA Modules:
  0.0 126.8 jit_solution(5748556177137140703)
XLA Ops:
  0.6 116.7 %shard_map.160 = (f32[512,768]{1,0:T(8,128)}, f32[512,768]{1,0:T(8,128)}, bf16[512,768]{1,0:T(8,128)(2,1)}, bf16[512,768]{1,0:T(8,128)(2,1)}, f32[1,512]{1,0:T(1...) custom-call(bf16[512,2048]{1,0:T(8,128)(2,1)} %bitcast.6, ...), custom_call_target="tpu_custom_call" | custom-call | tf_op jit(solution)/shard_map/pallas_call | solution.py:430
  117.3 0.0 copy-start
  117.3 2.8 %copy.27 = f32[512,768]{1,0:T(8,128)} copy(f32[512,768]{1,0:T(8,128)} %get-tuple-element.36) | data formatting | bytes 3145728
  120.1 0.0 copy-done
  120.1 0.0 copy-start.3
  120.1 0.0 copy-start.2
  120.1 1.1 copy.28
  121.2 0.5 copy-done.3
  121.8 0.0 copy-start.7
  121.8 0.0 copy-start.5
  121.8 0.0 copy-start.6
  121.8 0.0 copy-start.4
  121.8 0.0 copy-start.1
  121.8 0.9 copy.29
  122.7 0.0 copy-done.2
  122.7 0.9 copy.30
  123.6 0.0 copy-done.7
  123.6 0.6 copy.31
  124.1 0.0 copy-done.5
  124.1 0.6 copy.32
  124.7 0.0 copy-done.6
  124.7 0.6 copy.33
  125.3 0.0 copy-done.4
  125.3 0.6 copy.34
  125.9 0.0 copy-done.1
  125.9 0.9 copy.35
Async XLA Ops:
  117.3 2.8 %copy-start = (f32[512,768]{1,0:T(8,128)S(1)}, f32[512,768]{1,0:T(8,128)}, u32[]{:S(2)}) copy-start(f32[512,768]{1,0:T(8,128)} %get-tuple-element.37) | copy-start | bytes 4718596
  120.1 1.7 %copy-start.3 = (bf16[512,768]{1,0:T(8,128)(2,1)S(1)}, bf16[512,768]{1,0:T(8,128)(2,1)}, u32[]{:S(2)}) copy-start(bf16[512,768]{1,0:T(8,128)(2,1)} %get-tuple-element.20) | copy-start | bytes 2359300
  120.1 2.6 %copy-start.2 = (bf16[512,768]{1,0:T(8,128)(2,1)S(1)}, bf16[512,768]{1,0:T(8,128)(2,1)}, u32[]{:S(2)}) copy-start(bf16[512,768]{1,0:T(8,128)(2,1)} %get-tuple-element.21) | copy-start | bytes 2359300
  121.8 1.8 %copy-start.7 = (f32[1,512]{1,0:T(1,128)S(1)}, f32[1,512]{1,0:T(1,128)}, u32[]{:S(2)}) copy-start(f32[1,512]{1,0:T(1,128)} %get-tuple-element.40) | copy-start | bytes 6148
  121.8 2.4 %copy-start.5 = (f32[1,768]{1,0:T(1,128)S(1)}, f32[1,768]{1,0:T(1,128)}, u32[]{:S(2)}) copy-start(f32[1,768]{1,0:T(1,128)} %get-tuple-element.41) | copy-start | bytes 9220
  121.8 2.9 %copy-start.6 = (f32[1,512]{1,0:T(1,128)S(1)}, f32[1,512]{1,0:T(1,128)}, u32[]{:S(2)}) copy-start(f32[1,512]{1,0:T(1,128)} %get-tuple-element.42) | copy-start | bytes 6148
  121.8 3.5 %copy-start.4 = (f32[1,768]{1,0:T(1,128)S(1)}, f32[1,768]{1,0:T(1,128)}, u32[]{:S(2)}) copy-start(f32[1,768]{1,0:T(1,128)} %get-tuple-element.43) | copy-start | bytes 9220
  121.8 4.1 %copy-start.1 = (bf16[512,768]{1,0:T(8,128)(2,1)S(1)}, bf16[512,768]{1,0:T(8,128)(2,1)}, u32[]{:S(2)}) copy-start(bf16[512,768]{1,0:T(8,128)(2,1)} %get-tuple-element.26) | copy-start | bytes 2359300

commit v2 on v1

--- a/solution.py
+++ b/solution.py
@@ -32,7 +32,7 @@
 def kernel(
     n, G, S, R, PR, NP,
     x_hbm, c_hbm, w_hbm, m_hbm, q_hbm, frm, fcm, srm, scm,
-    o_w, o_m, o_fs, o_ss, o_frm, o_fcm, o_srm, o_scm, o_k,
+    o_a, o_fs, o_ss, o_frm, o_fcm, o_srm, o_scm, o_k,
     x, ct, w, m, q, tb, rb, pb, rp, av, wf, fn, sn, acc, fcol, scol, frn, srn, ca, cb, cmb,
     ld, ts, tr, ps, pr, as_, ar, gs, gr, hs, hr, cs, cr,
 ):
@@ -249,11 +249,11 @@
 
         def tile(i, carry):
             place = pl.ds(pl.multiple_of(s * R + i * TILE, TILE), TILE)
-            averaged = av[s, pl.ds(pl.multiple_of(i * TILE, TILE), TILE), :].astype(f32)
+            sent = av[s, pl.ds(pl.multiple_of(i * TILE, TILE), TILE), :]
+            o_a[place, :] = sent
+            averaged = sent.astype(f32)
             momentum = outer_beta * m[place, :] + averaged
             fresh = w[place, :].astype(f32) - outer_rate * (averaged + outer_beta * momentum)
-            o_m[place, :] = momentum
-            o_w[place, :] = fresh
             wf[z, place, :] = fresh.astype(bf16)
             return carry
 
@@ -413,6 +413,16 @@
         lax.fori_loop(0, G, plane, 0)
     for d in range(1, n):
         column_max(d, other_z).wait_send()
+
+
+def finish(avg, w, m, *refs):
+    o_w, o_m = refs[7:9]
+    averaged = avg[...].astype(f32)
+    momentum = outer_beta * m[...] + averaged
+    o_m[...] = momentum
+    o_w[...] = w[...].astype(f32) - outer_rate * (averaged + outer_beta * momentum)
+    for src, dst in zip(refs[:7], refs[9:]):
+        dst[...] = src[...]
 
 
 def local(x, ct, w, m, q, frm, fcm, srm, scm):
@@ -430,14 +440,13 @@
     outs = pl.pallas_call(
         functools.partial(kernel, n, G, S, R, PR, NP),
         out_shape=(
-            shape((rows, C), f32), shape((rows, C), f32),
-            shape((rows, C), bf16), shape((rows, C), bf16),
+            shape((rows, C), bf16), shape((rows, C), bf16), shape((rows, C), bf16),
             shape((1, rows), f32), shape((1, C), f32),
             shape((1, rows), f32), shape((1, C), f32),
             shape((T, C), bf16),
         ),
         in_specs=[hbm] * 5 + [vmem] * 4,
-        out_specs=(vmem,) * 9,
+        out_specs=(vmem,) * 8,
         scratch_shapes=[
             pltpu.VMEM((T, K), bf16), pltpu.VMEM((T, C), bf16), pltpu.VMEM((rows, C), bf16),
             pltpu.VMEM((rows, C), f32), pltpu.VMEM((rows, C), jnp.int32),
@@ -456,7 +465,25 @@
             collective_id=0, has_side_effects=True, vmem_limit_bytes=60 * 1024 * 1024
         ),
     )(x[0], ct[0], w, m, q[0], frm, fcm, srm, scm)
-    new_w, new_m, fs, ss, nfr, nfc, nsr, nsc, keys = outs
+    avg, fs, ss, nfr, nfc, nsr, nsc, keys = outs
+    steps = 4
+    high = pl.BlockSpec((rows // steps, C), lambda i: (i, 0))
+    tall = pl.BlockSpec((T // steps, C), lambda i: (i, 0))
+    wide = pl.BlockSpec((1, rows), lambda i: (0, 0))
+    flat = pl.BlockSpec((1, C), lambda i: (0, 0))
+    blocks = (high, high, tall, wide, flat, wide, flat)
+    new_w, new_m, fs, ss, keys, nfr, nfc, nsr, nsc = pl.pallas_call(
+        finish,
+        grid=(steps,),
+        out_shape=(
+            shape((rows, C), f32), shape((rows, C), f32),
+            shape((rows, C), bf16), shape((rows, C), bf16), shape((T, C), bf16),
+            shape((1, rows), f32), shape((1, C), f32),
+            shape((1, rows), f32), shape((1, C), f32),
+        ),
+        in_specs=(high,) * 3 + blocks,
+        out_specs=(high,) * 2 + blocks,
+    )(avg, w, m, fs, ss, keys, nfr, nfc, nsr, nsc)
     return new_w, new_m, fs[None], ss[None], nfr, nfc, nsr, nsc, keys[None]
 
 

time: 127 us -> 122 us (0.961)
  local copies, waits for them, and re-layouts: 9.42 us -> 0 us
  Pallas kernels: 117 us -> 121 us
    unnamed x25 -> x0, local copies, waits for them, and re-layouts: 9.42 us -> none
    pallas_call x0 -> x1, Pallas kernels: none -> 5.57 us  [local(): pl.pallas_call(finish, grid=(steps,), out_shape=(shape((rows, C), f32), s...]
where the time goes in v2:
time: 122 us
  Pallas kernels  121 us (99%)
    pallas_call x1, Pallas kernels, local(): pl.pallas_call(functools.partial(kernel, n, G, S, R, PR, NP), out_shape=(...  116 us
    pallas_call x1, Pallas kernels, local(): pl.pallas_call(finish, grid=(steps,), out_shape=(shape((rows, C), f32), s...  5.57 us

profile of v2, /device:TPU:0, one launch (start us, length us, event | category | flops | bytes accessed | tf_op | source)
XLA Modules:
  0.0 122.1 jit_solution(7599327422034823915)
XLA Ops:
  0.6 115.9 %shard_map.160 = (bf16[512,768]{1,0:T(8,128)(2,1)}, bf16[512,768]{1,0:T(8,128)(2,1)}, bf16[512,768]{1,0:T(8,128)(2,1)}, f32[1,512]{1,0:T(1,128)}, f32[1,768]{1,0...) custom-call(bf16[512,2048]{1,0:T(8,128)(2,1)} %bitcast.6, bf16[512,768]{1,0:T(8,128)(2,1)} %bitcast.8, ...), custom_call_target="tpu_custom_call" | custom-call | tf_op jit(solution)/shard_map/pallas_call | solution.py:440
  116.5 5.6 %shard_map.161 = (f32[512,768]{1,0:T(8,128)}, f32[512,768]{1,0:T(8,128)}, bf16[512,768]{1,0:T(8,128)(2,1)}, bf16[512,768]{1,0:T(8,128)(2,1)}, bf16[512,768]{1,0:...) custom-call(bf16[512,768]{1,0:T(8,128)(2,1)} %get-tuple-element.26.avg, ...), custom_call_target="tpu_custom_call" | custom-call | tf_op jit(solution)/shard_map/pallas_call | solution.py:475
